TPU v7x, 256 devices: a whole 4x4x8 slice. The times are simulated.
256 devices in a mesh: grp: 32 (over y, z_lo, core), dev: 8 (over x, z_hi).
Axes of the slice: x: 4, y: 4, z: 8 (z_hi: 2, z_lo: 4; z = z_hi * 4 + z_lo), core: 2. Of those that a mesh axis runs over, the one named last changes fastest.
Arguments:
- stack: bfloat16 [608, 256, 2048], P('grp', None, 'dev'), may hold values from -12 to 12
- network: int32 [608, 2], replicated, may hold values from 0 to 149, as said below
- bands: int32 [149], replicated, may hold values from 1 to 8
Outputs:
- deramped: bfloat16 [149, 256, 2048], P(None, 'grp', 'dev')
- misfit: float32 [256, 2048], P('grp', 'dev')
- spectrum: float32 [2, 149, 15, 15], replicated
Inputs may be any that keep to these rules, and one draw needn't show every extreme that they name: `network`: each row holds a reference date and a later secondary date, both below 150; every pair of consecutive dates is some row.
All inputs are finite; a program needn't handle non-finite values.
Results may differ from a plain program's by a relative error of at most 0.005.
Values may be sent and summed in bfloat16 or wider, within the bound.
No kernel may reach another device: no remote copies, remote signals or barrier semaphores. Data moves between devices by JAX's collectives and lax.ppermute only.
A program may use at most 128 MiB of HBM per device.

v0:
```python
import math
import jax
import jax.numpy as jnp
import numpy as np
from jax import lax
from jax.sharding import PartitionSpec as P

BAND = 8
FREQS = 2 * BAND - 1
HIGH = lax.Precision.HIGHEST


def design_of(network, solved):
    dates = jnp.arange(1, solved + 1, dtype=jnp.int32)
    return (network[:, 1:2] == dates[None, :]).astype(jnp.float32) - (
        network[:, 0:1] == dates[None, :]
    ).astype(jnp.float32)


def build_inverse(network, solved):
    design = design_of(network, solved)
    normal = jnp.dot(design.T, design, precision=HIGH)
    factor = jnp.linalg.cholesky(normal)
    pinv = jax.scipy.linalg.cho_solve((factor, True), design.T)
    return (pinv.astype(jnp.bfloat16), design.astype(jnp.bfloat16))


def basis(positions, length):
    index = jnp.arange(FREQS, dtype=jnp.int32)
    step = jnp.where(index < BAND, index, index - (BAND - 1))
    turns = positions[:, None] * step[None, :] % length
    angle = turns.astype(jnp.float32) * (2.0 * math.pi / length)
    return jnp.where(index[None, :] < BAND, jnp.cos(angle), jnp.sin(angle))


def mirror():
    out = np.zeros((FREQS, FREQS, 2, FREQS, FREQS), np.float32)
    for k in range(FREQS):
        for l in range(FREQS):
            fk, fl = (k - (BAND - 1), l - (BAND - 1))
            ck, cl = (abs(fk), abs(fl))
            sk, sl = (abs(fk) + BAND - 1, abs(fl) + BAND - 1)
            gk, gl = (np.sign(fk), np.sign(fl))
            out[k, l, 0, ck, cl] += 1
            if gk * gl:
                out[k, l, 0, sk, sl] -= gk * gl
            if gk:
                out[k, l, 1, sk, cl] -= gk
            if gl:
                out[k, l, 1, ck, sl] -= gl
    return out.reshape(FREQS * FREQS * 2, FREQS * FREQS)


def on_device(stack, network, bands):
    solved = bands.shape[0]
    groups = lax.axis_size("grp")
    held, rows_all, col_dev = stack.shape
    row_dev = rows_all // groups
    cols_all = col_dev * lax.axis_size("dev")
    pixels = row_dev * col_dev
    packed = stack.reshape(held, groups, row_dev, col_dev).transpose(1, 0, 2, 3)
    block = lax.all_to_all(packed, "grp", 0, 0, tiled=True)
    rows = basis(jnp.arange(rows_all, dtype=jnp.int32), rows_all)
    cols = basis(lax.axis_index("dev") * col_dev + jnp.arange(col_dev, dtype=jnp.int32), cols_all)
    wide = stack.astype(jnp.float32)
    half = jnp.einsum("ihw,ha->iaw", wide, rows, precision=HIGH)
    local = jnp.einsum("iaw,wb->iab", half, cols, precision=HIGH)
    local = local.reshape(held, FREQS * FREQS)
    summed = lax.psum(local, "dev")
    every = lax.all_gather(summed, "grp", axis=0, tiled=True)
    pinv, design = build_inverse(network, solved)
    scale = 1.0 / (rows_all * cols_all)
    coef = scale * lax.dot_general(
        every, pinv.astype(jnp.float32), (((0,), (1,)), ((), ())), precision=HIGH
    )
    index = np.arange(FREQS)
    step = np.where(index < BAND, index, index - (BAND - 1))
    weight = np.where(step == 0, 1.0, 2.0)
    kmax = np.maximum(step[:, None], step[None, :]).reshape(-1)
    both = (weight[:, None] * weight[None, :]).reshape(-1).astype(np.float32)
    masked = jnp.where(jnp.asarray(kmax)[:, None] < bands[None, :], coef, 0.0)
    signed = jnp.dot(jnp.asarray(mirror()), masked, precision=HIGH)
    spectrum = signed.reshape(FREQS, FREQS, 2, solved).transpose(2, 3, 0, 1)
    row_here = basis(
        lax.axis_index("grp") * row_dev + jnp.arange(row_dev, dtype=jnp.int32), rows_all
    )
    waves = (row_here.T[:, None, :, None] * cols.T[None, :, None, :]).reshape(FREQS * FREQS, pixels)
    ramp = lax.dot_general(
        masked * jnp.asarray(both)[:, None], waves, (((0,), (0,)), ((), ())), precision=HIGH
    )
    flat = block.reshape(held * groups, pixels)
    series = jnp.dot(pinv, flat, preferred_element_type=jnp.float32)
    deramped = (series - ramp).astype(jnp.bfloat16).reshape(solved, row_dev, col_dev)
    model = jnp.dot(design, series.astype(jnp.bfloat16), preferred_element_type=jnp.float32)
    resid = flat.astype(jnp.float32) - model
    misfit = jnp.sqrt(jnp.mean(resid * resid, axis=0) + 1e-06).reshape(row_dev, col_dev)
    return (deramped, misfit, spectrum)


def solution(mesh):
    return jax.shard_map(
        on_device,
        mesh=mesh,
        in_specs=(P("grp", None, "dev"), P(), P()),
        out_specs=(P(None, "grp", "dev"), P("grp", "dev"), P()),
        check_vma=False,
    )
```

profile of v0, /device:TPU:1, one launch (start us, length us, event | category | flops | bytes accessed | tf_op | source)
XLA Modules:
  0.0 182.2 jit_solution(6894326143020125078)
XLA Ops:
  0.6 0.0 copy-start
  0.6 1.7 copy-done
  2.3 1.6 copy_bitcast_fusion
  4.0 10.4 %all-to-all-start = ((bf16[32,19,8,256]{3,2,1,0:T(8,128)(2,1)}), bf16[32,19,8,256]{3,2,1,0:T(8,128)(2,1)}, u32[]{:S(2)}, u32[]{:S(2)}) async-start(bf16[32,19,8,256]{3,2,1,0:T(8,128)(2,1)} %copy_bitcast_fusion), calls=%async_computation | async-start | bytes 4980736 | tf_op jit(solution)/shard_map/all_to_all | solution.py:62
  14.4 1.5 fusion.4
  15.9 0.1 copy.17
  16.1 11.7 %cholesky.51 = f32[128,128]{1,0:T(8,128)S(1)} custom-call(f32[128,128]{1,0:T(8,128)S(1)} %cholesky.124), custom_call_target="Cholesky" | custom-call | tf_op jit(solution)/shard_map/jit(cholesky)/cholesky | solution.py:23
  27.8 9.8 %custom-call.18 = f32[1,128,128]{1,2,0:T(8,128)S(1)} custom-call(f32[1,128,128]{2,1,0:T(8,128)S(1)} %get-tuple-element.26), custom_call_target="InvertDiagBlocksLowerTriangular" | custom-call | tf_op jit(solution)/shard_map/jit(cholesky)/cholesky | solution.py:23
  37.7 0.2 constant_dynamic-update-slice_fusion.1
  37.8 0.2 convolution_subtract_fusion.3
  38.0 1.9 %cholesky.110 = f32[21,21]{1,0:T(8,128)S(1)} custom-call(f32[21,21]{1,0:T(8,128)S(1)} %convolution_subtract_fusion.3), custom_call_target="Cholesky" | custom-call | tf_op jit(solution)/shard_map/jit(cholesky)/cholesky | solution.py:23
  39.9 0.6 compare_reduce_fusion
  40.6 0.6 compare_reduce_fusion.1
  42.6 0.1 fusion.20
  42.7 19.9 %custom-call.19 = f32[2,128,128]{1,2,0:T(8,128)S(1)} custom-call(f32[2,128,128]{2,1,0:T(8,128)S(1)} %pad_maximum_fusion.3), custom_call_target="InvertDiagBlocksLowerTriangular" | custom-call | tf_op jit(solution)/shard_map/jit(_cho_solve)/triangular_solve | solution.py:24
  62.6 0.1 convert_subtract_fusion.2
  62.7 0.7 fusion.7
  63.4 0.7 copy-done.2
  64.2 0.4 convolution_subtract_fusion.2
  64.6 0.3 fusion.53
  64.8 0.2 fusion.82
  65.0 0.2 copy.18
  65.3 1.2 convolution_bitcast_fusion
  66.5 0.5 fusion.32
  67.0 0.1 reshape.205
  67.1 45.8 %psum.7 = f32[19,225]{1,0:T(8,128)S(1)} all-reduce(f32[19,225]{1,0:T(8,128)S(1)} %reshape.205), channel_id=1, replica_groups=mesh['grp'=32,'dev'=8] {'dev'}, use_global_device_ids=true, to_apply=%region_4.5 | all-reduce | flops 4275 | bytes 34200 | tf_op jit(solution)/shard_map/psum | solution.py:69
  112.9 53.9 %all-gather = f32[32,19,225]{2,1,0:T(8,128)S(1)} all-gather(f32[1,19,225]{2,1,0:T(8,128)S(1)} %bitcast.72), channel_id=1, replica_groups=mesh['grp'=32,'dev'=8] {'grp'}, dimensions={0}, use_global_device_ids=true | all-gather | bytes 564300 | tf_op jit(solution)/shard_map/all_gather | solution.py:70
  166.8 0.9 reshape.238
  167.7 0.1 sine_select_fusion.1
  167.8 0.2 sine_select_fusion
  168.0 0.2 broadcast_multiply_fusion
  168.2 0.1 pad.23
  168.4 0.0 copy-start.12
  168.4 0.0 copy-start.5
  168.4 2.1 %copy.23 = f32[29,8,8,256]{3,1,2,0:T(8,128)} copy(f32[29,8,8,256]{3,2,1,0:T(8,128)S(1)} %bitcast.67) | data formatting | bytes 3801088
  170.5 1.4 convolution_subtract_fusion.1
  171.9 0.4 convolution_convert_fusion
  172.3 0.5 fusion.1
  172.9 0.5 fusion.83
  173.4 1.0 reshape.207
  174.5 2.5 %copy.22 = bf16[76,8,8,256]{3,1,2,0:T(8,128)(2,1)S(1)} copy(bf16[76,8,8,256]{3,2,1,0:T(8,128)(2,1)} %bitcast.15) | data formatting | bytes 4980736
  177.0 0.7 fusion.16
  177.7 1.0 multiply_reduce_fusion
  178.7 0.5 copy-done.1
  179.2 1.3 fusion
  180.5 0.1 copy.24
  180.7 0.9 slice.94
  181.6 0.6 sqrt.8
  (38 shorter events, 0.3 us)
Async XLA Ops:
  0.6 1.7 copy-start
  4.0 10.4 %copy-start.9 = (s32[608,2]{0,1:T(2,128)S(1)}, s32[608,2]{0,1:T(2,128)}, u32[]{:S(2)}) copy-start(s32[608,2]{0,1:T(2,128)} %param.7) | copy-start | bytes 14596
  4.0 170.5 %all-to-all-start = ((bf16[32,19,8,256]{3,2,1,0:T(8,128)(2,1)}), bf16[32,19,8,256]{3,2,1,0:T(8,128)(2,1)}, u32[]{:S(2)}, u32[]{:S(2)}) async-start(bf16[32,19,8,256]{3,2,1,0:T(8,128)(2,1)} %copy_bitcast_fusion), calls=%async_computation | async-start | bytes 4980736 | tf_op jit(solution)/shard_map/all_to_all | solution.py:62
  42.5 23.9 %copy-start.6 = (f32[149,149]{1,0:T(8,128)}, f32[149,149]{1,0:T(8,128)S(1)}, u32[]{:S(2)}) copy-start(f32[149,149]{1,0:T(8,128)S(1)} %select_select_fusion) | copy-start | bytes 266416
  62.6 2.7 %copy-start.7 = (f32[2,128,128]{1,2,0:T(8,128)}, f32[2,128,128]{1,2,0:T(8,128)S(1)}, u32[]{:S(2)}) copy-start(f32[2,128,128]{1,2,0:T(8,128)S(1)} %custom-call.19) | copy-start | bytes 393220
  63.4 0.7 copy-start.2
  168.3 2.2 %copy-start.3 = (f32[128,608]{0,1:T(8,128)S(1)}, f32[128,608]{0,1:T(8,128)}, u32[]{:S(2)}) copy-start(f32[128,608]{0,1:T(8,128)} %copy-done.2) | copy-start | bytes 933892
  168.3 3.5 %copy-start.8 = (f32[2,128,128]{1,2,0:T(8,128)S(1)}, f32[2,128,128]{1,2,0:T(8,128)}, u32[]{:S(2)}) copy-start(f32[2,128,128]{1,2,0:T(8,128)} %copy-done.7) | copy-start | bytes 393220
  168.4 4.0 %copy-start.4 = (f32[608,225]{1,0:T(8,128)S(1)}, f32[608,225]{1,0:T(8,128)}, u32[]{:S(2)}) copy-start(f32[608,225]{1,0:T(8,128)} %reshape.238) | copy-start | bytes 1641604
  168.4 4.0 %copy-start.11 = (s32[149]{0:T(256)S(1)}, s32[149]{0:T(256)}, u32[]{:S(2)}) copy-start(s32[149]{0:T(256)} %param.8) | copy-start | bytes 1792
  168.4 4.0 %copy-start.12 = (s32[225]{0:T(256)S(1)}, s32[225]{0:T(256)}, u32[]{:S(2)}) copy-start(s32[225]{0:T(256)} %constant.175.clone) | copy-start | bytes 2704
  168.4 4.5 %copy-start.5 = (f32[450,225]{1,0:T(8,128)S(1)}, f32[450,225]{1,0:T(8,128)}, u32[]{:S(2)}) copy-start(f32[450,225]{1,0:T(8,128)} %constant.176.clone) | copy-start | bytes 1215004
  177.7 1.5 copy-start.1
  177.7 1.5 copy-start.10
where the time goes:
time: 183 us; the launch traced here: 182 us
  blocking collectives  99.7 us (54%)
  other arithmetic  45.4 us (25%)
  local copies, waits for them, and re-layouts  13.4 us (7%)
  matrix products  11 us (6%)
  starting transfers between devices  10.4 us (6%)
  between operations  2.38 us (1%)
    all_gather x1, blocking collectives, on_device(): every = lax.all_gather(summed, 'grp', axis=0, tiled=True)  53.9 us
    psum x1, blocking collectives, on_device(): summed = lax.psum(local, 'dev')  45.8 us
    another operation x7, other arithmetic, build_inverse(): factor = jnp.linalg.cholesky(normal)  24.8 us
    another operation x6, other arithmetic, build_inverse(): pinv = jax.scipy.linalg.cho_solve((factor, True), design.T)  20 us
    all_to_all x1, starting transfers between devices, on_device(): block = lax.all_to_all(packed, 'grp', 0, 0, tiled=True)  10.4 us
    unnamed x31, local copies, waits for them, and re-layouts  8.8 us
  transfers between devices with their start and end apart: 1, of which 0 were waited for; matrix products, arithmetic and copies ran while one was open for 32% of the time, Pallas kernels for 0%

commit v1 on v0

--- a/solution.py
+++ b/solution.py
@@ -4,6 +4,7 @@
 import numpy as np
 from jax import lax
 from jax.sharding import PartitionSpec as P
+from jax.lax import all_gather
 
 BAND = 8
 FREQS = 2 * BAND - 1
@@ -66,7 +67,7 @@
     half = jnp.einsum("ihw,ha->iaw", wide, rows, precision=HIGH)
     local = jnp.einsum("iaw,wb->iab", half, cols, precision=HIGH)
     local = local.reshape(held, FREQS * FREQS)
-    summed = lax.psum(local, "dev")
+    summed = jnp.sum(all_gather(local, "dev"), axis=0)
     every = lax.all_gather(summed, "grp", axis=0, tiled=True)
     pinv, design = build_inverse(network, solved)
     scale = 1.0 / (rows_all * cols_all)

time: 183 us -> 174 us (0.951)
  blocking collectives: 99.7 us -> 91 us
    psum x1 -> x0, blocking collectives: 45.8 us -> none  [on_device(): summed = lax.psum(local, 'dev')]
    all_gather x0 -> x1, blocking collectives: none -> 38.2 us  [on_device(): summed = jnp.sum(all_gather(local, 'dev'), axis=0)]
  transfers between devices with their start and end apart: 1 -> 1, of which waited for: 0 -> 0; matrix products, arithmetic and copies ran while one was open for 32% -> 33% of each run, Pallas kernels for 0% -> 0%
where the time goes in v1:
time: 174 us
  blocking collectives  91 us (52%)
  other arithmetic  45.5 us (26%)
  local copies, waits for them, and re-layouts  13.4 us (8%)
  matrix products  11 us (6%)
  starting transfers between devices  10.4 us (6%)
  between operations  2.38 us (1%)
    all_gather x1, blocking collectives, on_device(): every = lax.all_gather(summed, 'grp', axis=0, tiled=True)  52.8 us
    all_gather x1, blocking collectives, on_device(): summed = jnp.sum(all_gather(local, 'dev'), axis=0)  38.2 us
    another operation x7, other arithmetic, build_inverse(): factor = jnp.linalg.cholesky(normal)  24.8 us
    another operation x6, other arithmetic, build_inverse(): pinv = jax.scipy.linalg.cho_solve((factor, True), design.T)  20 us
    all_to_all x1, starting transfers between devices, on_device(): block = lax.all_to_all(packed, 'grp', 0, 0, tiled=True)  10.4 us
    unnamed x31, local copies, waits for them, and re-layouts  8.8 us
  transfers between devices with their start and end apart: 1, of which 0 were waited for; matrix products, arithmetic and copies ran while one was open for 33% of the time, Pallas kernels for 0%

profile of v1, /device:TPU:1, one launch (start us, length us, event | category | flops | bytes accessed | tf_op | source)
XLA Modules:
  0.0 173.5 jit_solution(6064632771752645810)
XLA Ops:
  0.6 0.0 copy-start
  0.6 1.7 copy-done
  2.3 1.6 copy_bitcast_fusion
  4.0 10.4 %all-to-all-start = ((bf16[32,19,8,256]{3,2,1,0:T(8,128)(2,1)}), bf16[32,19,8,256]{3,2,1,0:T(8,128)(2,1)}, u32[]{:S(2)}, u32[]{:S(2)}) async-start(bf16[32,19,8,256]{3,2,1,0:T(8,128)(2,1)} %copy_bitcast_fusion), calls=%async_computation | async-start | bytes 4980736 | tf_op jit(solution)/shard_map/all_to_all | solution.py:63
  14.4 1.5 fusion.4
  15.9 0.1 copy.17
  16.1 11.7 %cholesky.51 = f32[128,128]{1,0:T(8,128)S(1)} custom-call(f32[128,128]{1,0:T(8,128)S(1)} %cholesky.124), custom_call_target="Cholesky" | custom-call | tf_op jit(solution)/shard_map/jit(cholesky)/cholesky | solution.py:24
  27.8 9.8 %custom-call.18 = f32[1,128,128]{1,2,0:T(8,128)S(1)} custom-call(f32[1,128,128]{2,1,0:T(8,128)S(1)} %get-tuple-element.26), custom_call_target="InvertDiagBlocksLowerTriangular" | custom-call | tf_op jit(solution)/shard_map/jit(cholesky)/cholesky | solution.py:24
  37.7 0.2 constant_dynamic-update-slice_fusion.1
  37.8 0.2 convolution_subtract_fusion.3
  38.0 1.9 %cholesky.110 = f32[21,21]{1,0:T(8,128)S(1)} custom-call(f32[21,21]{1,0:T(8,128)S(1)} %convolution_subtract_fusion.3), custom_call_target="Cholesky" | custom-call | tf_op jit(solution)/shard_map/jit(cholesky)/cholesky | solution.py:24
  39.9 0.6 compare_reduce_fusion
  40.6 0.6 compare_reduce_fusion.1
  42.6 0.1 fusion.20
  42.7 19.9 %custom-call.19 = f32[2,128,128]{1,2,0:T(8,128)S(1)} custom-call(f32[2,128,128]{2,1,0:T(8,128)S(1)} %pad_maximum_fusion.3), custom_call_target="InvertDiagBlocksLowerTriangular" | custom-call | tf_op jit(solution)/shard_map/jit(_cho_solve)/triangular_solve | solution.py:25
  62.6 0.1 convert_subtract_fusion.2
  62.7 0.7 fusion.7
  63.4 0.7 copy-done.2
  64.2 0.4 convolution_subtract_fusion.2
  64.6 0.3 fusion.53
  64.8 0.2 fusion.82
  65.0 0.2 copy.18
  65.3 1.2 convolution_bitcast_fusion
  66.5 0.5 fusion.32
  67.0 0.1 all_gather_reshape.3
  67.1 38.2 %all_gather.6 = f32[8,19,225]{2,1,0:T(8,128)S(1)} all-gather(f32[1,19,225]{2,1,0:T(8,128)S(1)} %all_gather_reshape.3), channel_id=1, replica_groups=mesh['grp'=32,'dev'=8] {'dev'}, dimensions={0}, use_global_device_ids=true | all-gather | bytes 153900 | tf_op jit(solution)/shard_map/all_gather | solution.py:70
  105.4 52.8 %all-gather = f32[32,19,225]{2,1,0:T(8,128)S(1)} all-gather(f32[1,19,225]{2,1,0:T(8,128)S(1)} %bitcast.72), channel_id=1, replica_groups=mesh['grp'=32,'dev'=8] {'grp'}, dimensions={0}, use_global_device_ids=true | all-gather | bytes 564300 | tf_op jit(solution)/shard_map/all_gather | solution.py:71
  158.2 0.9 reshape.234
  159.1 0.1 sine_select_fusion.1
  159.2 0.2 sine_select_fusion
  159.4 0.2 broadcast_multiply_fusion
  159.6 0.1 pad.23
  159.7 0.0 copy-start.12
  159.7 0.0 copy-start.5
  159.8 2.1 %copy.23 = f32[29,8,8,256]{3,1,2,0:T(8,128)} copy(f32[29,8,8,256]{3,2,1,0:T(8,128)S(1)} %bitcast.67) | data formatting | bytes 3801088
  161.9 1.4 convolution_subtract_fusion.1
  163.3 0.4 convolution_convert_fusion
  163.7 0.5 fusion.1
  164.2 0.5 fusion.83
  164.8 1.0 reshape.203
  165.8 2.5 %copy.22 = bf16[76,8,8,256]{3,1,2,0:T(8,128)(2,1)S(1)} copy(bf16[76,8,8,256]{3,2,1,0:T(8,128)(2,1)} %bitcast.15) | data formatting | bytes 4980736
  168.4 0.7 fusion.16
  169.1 1.0 multiply_reduce_fusion
  170.0 0.5 copy-done.1
  170.6 1.3 fusion
  171.9 0.1 copy.24
  172.1 0.9 slice.94
  172.9 0.6 sqrt.8
  (39 shorter events, 0.3 us)
Async XLA Ops:
  0.6 1.7 copy-start
  4.0 10.4 %copy-start.9 = (s32[608,2]{0,1:T(2,128)S(1)}, s32[608,2]{0,1:T(2,128)}, u32[]{:S(2)}) copy-start(s32[608,2]{0,1:T(2,128)} %param.7) | copy-start | bytes 14596
  4.0 161.9 %all-to-all-start = ((bf16[32,19,8,256]{3,2,1,0:T(8,128)(2,1)}), bf16[32,19,8,256]{3,2,1,0:T(8,128)(2,1)}, u32[]{:S(2)}, u32[]{:S(2)}) async-start(bf16[32,19,8,256]{3,2,1,0:T(8,128)(2,1)} %copy_bitcast_fusion), calls=%async_computation | async-start | bytes 4980736 | tf_op jit(solution)/shard_map/all_to_all | solution.py:63
  42.5 23.9 %copy-start.6 = (f32[149,149]{1,0:T(8,128)}, f32[149,149]{1,0:T(8,128)S(1)}, u32[]{:S(2)}) copy-start(f32[149,149]{1,0:T(8,128)S(1)} %select_select_fusion) | copy-start | bytes 266416
  62.6 2.7 %copy-start.7 = (f32[2,128,128]{1,2,0:T(8,128)}, f32[2,128,128]{1,2,0:T(8,128)S(1)}, u32[]{:S(2)}) copy-start(f32[2,128,128]{1,2,0:T(8,128)S(1)} %custom-call.19) | copy-start | bytes 393220
  63.4 0.7 copy-start.2
  159.7 2.2 %copy-start.3 = (f32[128,608]{0,1:T(8,128)S(1)}, f32[128,608]{0,1:T(8,128)}, u32[]{:S(2)}) copy-start(f32[128,608]{0,1:T(8,128)} %copy-done.2) | copy-start | bytes 933892
  159.7 3.5 %copy-start.8 = (f32[2,128,128]{1,2,0:T(8,128)S(1)}, f32[2,128,128]{1,2,0:T(8,128)}, u32[]{:S(2)}) copy-start(f32[2,128,128]{1,2,0:T(8,128)} %copy-done.7) | copy-start | bytes 393220
  159.7 4.0 %copy-start.4 = (f32[608,225]{1,0:T(8,128)S(1)}, f32[608,225]{1,0:T(8,128)}, u32[]{:S(2)}) copy-start(f32[608,225]{1,0:T(8,128)} %reshape.234) | copy-start | bytes 1641604
  159.7 4.0 %copy-start.11 = (s32[149]{0:T(256)S(1)}, s32[149]{0:T(256)}, u32[]{:S(2)}) copy-start(s32[149]{0:T(256)} %param.8) | copy-start | bytes 1792
  159.7 4.0 %copy-start.12 = (s32[225]{0:T(256)S(1)}, s32[225]{0:T(256)}, u32[]{:S(2)}) copy-start(s32[225]{0:T(256)} %constant.175.clone) | copy-start | bytes 2704
  159.7 4.5 %copy-start.5 = (f32[450,225]{1,0:T(8,128)S(1)}, f32[450,225]{1,0:T(8,128)}, u32[]{:S(2)}) copy-start(f32[450,225]{1,0:T(8,128)} %constant.176.clone) | copy-start | bytes 1215004
  169.1 1.5 copy-start.1
  169.1 1.5 copy-start.10
